TPU v7x, 32 devices: a whole 2x2x4 slice. The times are simulated.
32 devices in a mesh: cuts: 4 (over z), row: 8 (over y, x, core).
Axes of the slice: x: 2, y: 2, z: 4, core: 2. Of those that a mesh axis runs over, the one named last changes fastest.
Arguments:
- eigvecs: float32 [16384, 2048], P('row', 'cuts'), may hold values from -1.2 to 1.2
- slice_counts: int32 [4], P('cuts'), may hold values from 256 to 512, as said below
- occ_index: int32 [2048], P('cuts'), may hold values from 0 to 63
- occ_levels: float32 [64], replicated, may hold values from 0 to 1
Outputs:
- slab: float32 [4096, 16384], P('cuts', 'row')
Inputs may be any that keep to these rules, and one draw needn't show every extreme that they name: `slice_counts`: some slice holds exactly 512 eigenvalues in every draw; the others at least half of that.
All inputs are finite; a program needn't handle non-finite values.
Results may differ from a plain program's by a relative error of at most 0.000062.
Values sent between devices are 32-bit elements; how exact they have to be, the bound alone decides.
No kernel may reach another device: no remote copies, remote signals or barrier semaphores. Data moves between devices by JAX's collectives and lax.ppermute only.
A program may use at most 128 MiB of HBM per device.

v0:
```python
import jax
import jax.numpy as jnp
from jax import lax
from jax.sharding import PartitionSpec as P

BLOCK = 1024
SLAB_SUB = 256
SLAB = 4096


def shards(eigvecs, slice_counts, occ_index, occ_levels):
    row_count = eigvecs.shape[0]
    slot_count = eigvecs.shape[1]
    level_ids = jnp.arange(occ_levels.shape[0], dtype=jnp.int32)
    one_hot = (occ_index[:, None] == level_ids[None, :]).astype(jnp.float32)
    values = jnp.dot(one_hot, occ_levels, precision=lax.Precision.HIGHEST)
    live = jnp.arange(slot_count, dtype=jnp.int32) < slice_counts[0]
    weights = jnp.where(live, values, jnp.float32(0.0))
    local_blocks = eigvecs.reshape(row_count // BLOCK, BLOCK, slot_count)[:, :SLAB_SUB, :]
    local_rows = local_blocks.reshape(-1, slot_count) * weights[None, :]
    cut_count = lax.axis_size("cuts")
    row_devices = lax.axis_size("row")
    owned = SLAB // cut_count
    strip = slot_count // row_devices
    spread = lax.all_to_all(local_rows.T, "row", split_axis=0, concat_axis=1, tiled=True)
    owners = lax.all_to_all(spread, "cuts", split_axis=1, concat_axis=0, tiled=True)
    panels = lax.all_gather(owners, "row", axis=0, tiled=True)
    panel = (
        panels.reshape(row_devices, cut_count, strip, owned)
        .transpose(1, 0, 2, 3)
        .reshape(cut_count * slot_count, owned)
    )
    return lax.dot_general(
        panel,
        lax.all_gather(eigvecs, "cuts", axis=1, tiled=True),
        (((0,), (1,)), ((), ())),
        precision=lax.Precision.HIGHEST,
        preferred_element_type=jnp.float32,
    )


def solution(mesh):
    return jax.shard_map(
        shards,
        mesh=mesh,
        in_specs=(P("row", "cuts"), P("cuts"), P("cuts"), P()),
        out_specs=P("cuts", "row"),
        check_vma=False,
    )
```

profile of v0, /device:TPU:0, one launch (start us, length us, event | category | flops | bytes accessed | tf_op | source)
XLA Modules:
  0.0 519.5 jit_solution(15764011367793498607)
XLA Ops:
  6.5 0.0 copy-start
  6.5 0.0 all-gather.3.cloned.1.call-start
  7.2 1.3 slice.4
  8.5 0.3 copy.14
  8.8 0.0 copy-done
  8.9 1.0 fusion
  9.9 0.2 broadcast_multiply_fusion
  10.0 20.3 %all_to_all.35 = f32[8,64,512]{2,1,0:T(8,128)S(1)} all-to-all(f32[8,64,512]{2,1,0:T(8,128)S(1)} %bitcast.24), channel_id=1, replica_groups=mesh['cuts'=4,'row'=8] {'row'}, dimensions={0} | all-to-all | bytes 2097152 | tf_op jit(solution)/shard_map/all_to_all | solution.py:25
  30.3 0.6 copy.10
  31.0 0.5 all_to_all.29
  31.5 0.6 copy.11
  32.1 29.9 %all_to_all.36 = f32[64,4,1024]{2,0,1:T(8,128)} all-to-all(f32[64,4,1024]{2,0,1:T(8,128)S(1)} %copy.11), channel_id=1, replica_groups=mesh['cuts'=4,'row'=8] {'cuts'}, dimensions={1} | all-to-all | bytes 2097152 | tf_op jit(solution)/shard_map/all_to_all | solution.py:26
  62.0 0.0 all-gather.3.cloned.1.call-update
  62.1 0.0 all-gather.5.cloned.1.call-start
  62.1 0.7 all-gather.5.cloned.1.call-update
  62.8 51.5 %all-gather.3.cloned.1.call-done = f32[2048,1024]{1,0:T(8,128)} async-done(((f32[256,1024]{1,0:T(8,128)}), f32[2048,1024]{1,0:T(8,128)}) %all-gather.3.cloned.1.call-update) | async-done | bytes 8388624 | tf_op jit(solution)/shard_map/all_gather | solution.py:27
  114.3 8.3 %copy.12 = f32[8,4,64,1024]{3,2,0,1:T(8,128)} copy(f32[8,4,64,1024]{3,2,1,0:T(8,128)} %bitcast.21) | data formatting | bytes 16777216 | tf_op jit(solution)/shard_map/reshape | solution.py:29
  122.6 280.1 %all-gather.5.cloned.1.call-done = f32[2048,2048]{1,0:T(8,128)} async-done(((f32[2048,512]{1,0:T(8,128)}), f32[2048,2048]{1,0:T(8,128)}) %all-gather.5.cloned.1.call-update) | async-done | bytes 16777232 | tf_op jit(solution)/shard_map/all_gather | solution.py:35
  402.7 110.0 %fusion.4 = f32[1024,2048]{1,0:T(8,128)} fusion(f32[2048,1024]{1,0:T(8,128)} %bitcast.22, f32[2048,2048]{1,0:T(8,128)} %all-gather.5.cloned.1.call-done), kind=kOutput, calls=%fused_computation.7 | convolution fusion | flops 51539607552 | bytes 33554432 | tf_op jit(solution)/shard_map/dot_general | solution.py:33
  (1 shorter events, 0.0 us)
Async XLA Ops:
  6.5 2.3 copy-start
  6.5 107.8 %all-gather.3.cloned.1.call-start = ((), (), s32[]{:S(2)}) async-start(), calls=%async_computation.2 | async-start | bytes 9437184 | tf_op jit(solution)/shard_map/all_gather | solution.py:27
  62.1 340.6 %all-gather.5.cloned.1.call-start = ((), (), s32[]{:S(2)}) async-start(), calls=%async_computation.3 | async-start | bytes 20971520 | tf_op jit(solution)/shard_map/all_gather | solution.py:35
Sparse Core Ops, SparseCore 0:
  62.2 52.0 all-gather.2
  115.9 286.7 all-gather.4
where the time goes:
time: 520 us; the launch traced here: 519 us
  waiting for transfers between devices  332 us (64%)
  matrix products  111 us (21%)
  blocking collectives  50.3 us (10%)
  between operations  14.1 us (3%)
  local copies, waits for them, and re-layouts  11.6 us (2%)
    all_gather x1, waiting for transfers between devices, shards(): lax.all_gather(eigvecs, 'cuts', axis=1, tiled=True)  280 us
    dot_general x1, matrix products, shards(): lax.dot_general(panel, lax.all_gather(eigvecs, 'cuts', axis=1, tiled=True...  110 us
    all_gather x1, waiting for transfers between devices, shards(): panels = lax.all_gather(owners, 'row', axis=0, tiled=True)  51.5 us
    all_to_all x1, blocking collectives, shards(): lax.all_to_all(spread, 'cuts', split_axis=1, concat_axis=0, tiled=True)  29.9 us
    all_to_all x1, blocking collectives, shards(): lax.all_to_all(local_rows.T, 'row', split_axis=0, concat_axis=1, tiled=True)  20.3 us
  transfers between devices with their start and end apart: 2, of which 2 were waited for; matrix products, arithmetic and copies ran while one was open for 2% of the time, Pallas kernels for 0%

commit v1 on v0

v1 whole, which is shorter than its diff:
```python
import functools

import jax
import jax.numpy as jnp
from jax import lax
from jax.experimental import pallas as pl
from jax.experimental.pallas import tpu as pltpu
from jax.sharding import PartitionSpec as P


BLOCK = 1024
SLAB_SUB = 256
TILE = 256
SIZES = (2, 1, 1, 1, 1)
STRIDE = 32
PIECES = 8


def slot_weights(slice_counts, occ_index, occ_levels):
    level_ids = jnp.arange(occ_levels.shape[0], dtype=jnp.int32)
    one_hot = (occ_index[:, None] == level_ids[None, :]).astype(jnp.float32)
    values = jnp.dot(one_hot, occ_levels, precision=lax.Precision.HIGHEST)
    live = jnp.arange(occ_index.shape[0], dtype=jnp.int32) < slice_counts[0]
    return jnp.where(live, values, jnp.float32(0.0))


def split(value):
    high = value.astype(jnp.bfloat16)
    return high, (value - high.astype(jnp.float32)).astype(jnp.bfloat16)


def product_kernel(shape, always, with_base, tiles, flag, rows_ref, *refs):
    parts = []
    for counts in shape:
        parts.append([])
        for count in counts:
            parts[-1].append(refs[:count])
            refs = refs[count:]
    out_ref, rows_f32, a_both, b_both, arrived = refs[int(with_base) :]
    step = pl.program_id(0)
    depth = parts[0][0][0].shape[1]
    pieces, height = rows_f32.shape[0], rows_f32.shape[1]

    def copy(i):
        at = pl.ds(pl.multiple_of(i * height, height), height)
        return pltpu.make_async_copy(rows_ref.at[at, :], rows_f32.at[i], arrived.at[i])

    def multiply():
        @pl.when(step == 0)
        def _():
            @pl.loop(0, pieces)
            def _(i):
                copy(i).start()

        for index, tile_parts in enumerate(parts):

            @pl.when(step == index)
            def _():
                for q, terms in enumerate(tile_parts):
                    at = slice(q * depth, (q + 1) * depth)

                    @pl.loop(0, TILE // STRIDE)
                    def _(j):
                        rows = pl.ds(pl.multiple_of(j * STRIDE, STRIDE), STRIDE)
                        value = functools.reduce(jnp.add, [term[rows, :] for term in terms])
                        b_both[0, rows, at], b_both[1, rows, at] = split(value)

        @pl.when(step == 0)
        def _():
            @pl.loop(0, pieces)
            def _(i):
                copy(i).wait()

                @pl.loop(0, height // STRIDE)
                def _(j):
                    at = pl.ds(pl.multiple_of(j * STRIDE, STRIDE), STRIDE)
                    to = pl.ds(pl.multiple_of(i * height + j * STRIDE, STRIDE), STRIDE)
                    a_both[0, to, :], a_both[1, to, :] = split(rows_f32[i, at, :])

        dims = (((1,), (1,)), ((), ()))
        dot = functools.partial(
            lax.dot_general, dimension_numbers=dims, preferred_element_type=jnp.float32
        )
        out_ref[...] = dot(a_both[0], b_both[0])

        @pl.loop(1, 3)
        def _(term):
            out_ref[...] += dot(a_both[term % 2], b_both[term // 2])

    if always:
        multiply()
    else:
        pl.when(flag[0] == 0)(multiply)


def product(rows, parts, flag, tiles, all_columns, always=False, base=None):
    owned, depth = rows.shape
    slots = parts[0][0][0][0].shape[1]
    shape = [[len(terms) for terms in tile_parts] for tile_parts in parts]
    operands = [rows]
    in_specs = [pl.BlockSpec(memory_space=pl.ANY)]
    for tile_parts in parts:
        for terms in tile_parts:
            for array, block in terms:
                operands.append(array)
                in_specs.append(
                    pl.BlockSpec(
                        (TILE, slots),
                        lambda i, t, f, block=block: (block, 0),
                        pipeline_mode=pl.Buffered(1),
                    )
                )
    aliases = {}
    if base is not None:
        aliases = {2 + len(operands): 0}
        in_specs.append(pl.BlockSpec(memory_space=pl.ANY))
        operands.append(base)
    return pl.pallas_call(
        functools.partial(product_kernel, shape, always, base is not None),
        grid_spec=pltpu.PrefetchScalarGridSpec(
            num_scalar_prefetch=2,
            grid=(len(tiles),),
            in_specs=in_specs,
            out_specs=pl.BlockSpec((owned, TILE), lambda i, t, f: (0, t[i])),
            scratch_shapes=[
                pltpu.VMEM((PIECES, owned // PIECES, depth), jnp.float32),
                pltpu.VMEM((2, owned, depth), jnp.bfloat16),
                pltpu.VMEM((2, TILE, depth), jnp.bfloat16),
                pltpu.SemaphoreType.DMA((PIECES,)),
            ],
        ),
        out_shape=jax.ShapeDtypeStruct((owned, all_columns), jnp.float32),
        input_output_aliases=aliases,
        cost_estimate=pl.CostEstimate(
            flops=6 * owned * TILE * len(tiles) * depth,
            bytes_accessed=4 * (owned * depth + TILE * len(tiles) * (depth + owned)),
            transcendentals=0,
        ),
        name="product",
    )(jnp.asarray(tiles, jnp.int32), flag, *operands)


def place_kernel(tiles, flag, base_ref, sent_ref, out_ref, held, done):
    @pl.when(flag[0] != 0)
    def _():
        for index, tile in enumerate(tiles):
            take = pltpu.make_async_copy(
                sent_ref.at[:, pl.ds(index * TILE, TILE)], held.at[index], done.at[index]
            )
            take.start()
        for index, tile in enumerate(tiles):
            pltpu.make_async_copy(
                sent_ref.at[:, pl.ds(index * TILE, TILE)], held.at[index], done.at[index]
            ).wait()
            pltpu.make_async_copy(
                held.at[index], out_ref.at[:, pl.ds(tile * TILE, TILE)], done.at[index]
            ).start()
        for index, tile in enumerate(tiles):
            pltpu.make_async_copy(
                held.at[index], out_ref.at[:, pl.ds(tile * TILE, TILE)], done.at[index]
            ).wait()


def place(base, sent, flag, tiles):
    owned = base.shape[0]
    hbm = pl.BlockSpec(memory_space=pl.ANY)
    return pl.pallas_call(
        functools.partial(place_kernel, tiles),
        in_specs=[pl.BlockSpec(memory_space=pltpu.SMEM), hbm, hbm],
        out_specs=hbm,
        scratch_shapes=[
            pltpu.VMEM((len(tiles), owned, TILE), jnp.float32),
            pltpu.SemaphoreType.DMA((len(tiles),)),
        ],
        out_shape=jax.ShapeDtypeStruct(base.shape, base.dtype),
        input_output_aliases={1: 0},
        cost_estimate=pl.CostEstimate(
            flops=0, bytes_accessed=8 * owned * TILE * len(tiles), transcendentals=0
        ),
        name="place",
    )(flag, base, sent)


def slab_block(eigvecs, slice_counts, occ_index, occ_levels):
    row_count, slot_count = eigvecs.shape
    cuts = lax.axis_size("cuts")
    row_devices = lax.axis_size("row")
    cut = lax.axis_index("cuts")
    last = cuts - 1
    turns = [0, 1, last] + list(range(2, last))
    at_end = ((cut == 0) | (cut == last)).astype(jnp.int32).reshape(1)

    weights = slot_weights(slice_counts, occ_index, occ_levels)
    blocks = eigvecs.reshape(row_count // BLOCK, BLOCK, slot_count)
    picked = blocks[:, :SLAB_SUB, :].reshape(-1, slot_count)
    halves = row_devices // cuts

    up, down = [picked], [picked]
    for step in range(1, cuts):
        up.append(lax.ppermute(up[-1], "cuts", [(i, i + 1) for i in range(step - 1, last)]))
        down.append(lax.ppermute(down[-1], "cuts", [(i + 1, i) for i in range(last - step + 1)]))
    every = [(picked,)] + [(up[turn], down[cuts - turn]) for turn in turns[1:]]

    def spread(rows):
        return lax.all_to_all(rows, "row", split_axis=0, concat_axis=0, tiled=True)

    def to_plane(strips, block):
        strip = strips.shape[0] // cuts
        return lax.dynamic_slice_in_dim(strips, block * strip, strip, axis=0)

    def gathered(wide):
        wide = wide.reshape(halves, wide.shape[0] // halves, wide.shape[1])
        wide = lax.all_gather(wide, "row", axis=1, tiled=True)
        return wide.reshape(-1, wide.shape[2])

    def end_of(plane):
        return jnp.where(plane == 1, 0, last)

    strips = spread(picked * weights[None, :])
    other, own = [to_plane(strips, end_of(cut))], [to_plane(strips, cut)]
    for turn in turns[1:]:
        pairs = [(i, (i + turn) % cuts) for i in range(cuts)]
        inner = [(i, j) for i, j in pairs if j in (1, last - 1)]
        piece = to_plane(strips, end_of((cut + turn) % cuts))
        other.append(lax.ppermute(piece, "cuts", inner))
        piece = to_plane(strips, (cut + turn) % cuts)
        own.append(lax.ppermute(piece, "cuts", pairs))
    other = gathered(jnp.concatenate(other, axis=1))
    own = gathered(jnp.concatenate(own, axis=1))

    groups, tile_parts = unpicked_groups(row_count), {}
    for group in groups:
        mine = jnp.concatenate([eigvecs[t * TILE : (t + 1) * TILE] for t in group], axis=0)
        parts = [mine]
        for turn in turns[1:]:
            pairs = [(i, (i + turn) % cuts) for i in range(cuts)]
            pairs = [(i, j) for i, j in pairs if 0 < j < last]
            parts.append(lax.ppermute(mine, "cuts", pairs))
        for block, tile in enumerate(group):
            tile_parts[tile] = [[(part, block)] for part in parts]
    sents = {}
    for tile, parts in tile_parts.items():
        served = product(other, [parts], at_end, [0], TILE)
        sents[tile] = lax.ppermute(served, "cuts", [(1, 0), (last - 1, last)])

    picked_tiles = [t for t in range(row_count // TILE) if (t * TILE) % BLOCK < SLAB_SUB]
    picked_parts = [
        [[(term, block) for term in terms] for terms in every] for block in range(len(picked_tiles))
    ]
    out = product(own, picked_parts, at_end, picked_tiles, row_count, always=True)
    for group in owned_groups(row_count):
        out = product(own, [tile_parts[t] for t in group], at_end, group, row_count, base=out)
    for tile, sent in sents.items():
        out = place(out, sent, at_end, [tile])
    return out


def unpicked_groups(row_count):
    tiles = [t for t in range(row_count // TILE) if (t * TILE) % BLOCK >= SLAB_SUB]
    groups = []
    for size in SIZES:
        groups.append(tiles[:size])
        tiles = tiles[size:]
    return [g for g in groups + [tiles] if g]


def owned_groups(row_count):
    tiles = [t for group in unpicked_groups(row_count) for t in group]
    return [tiles[i : i + 2] for i in range(0, len(tiles), 2)]


def solution(mesh):
    return jax.shard_map(
        slab_block,
        mesh=mesh,
        in_specs=(P("row", "cuts"), P("cuts"), P("cuts"), P()),
        out_specs=P("cuts", "row"),
        check_vma=False,
    )
```

time: 520 us -> 390 us (0.75)
  waiting for transfers between devices: 332 us -> 166 us
  starting transfers between devices: 0.04 us -> 134 us
  matrix products: 111 us -> 0.99 us
  Pallas kernels: 0 us -> 58.4 us
  blocking collectives: 50.3 us -> 0 us
    all_gather x2, waiting for transfers between devices: 332 us -> 0.01 us  [gathered(): wide = lax.all_gather(wide, 'row', axis=1, tiled=True)]
    ppermute x0 -> x33, waiting for transfers between devices: none -> 151 us  [the longest x6 85.7 us: slab_block(): sents[tile] = lax.ppermute(served, 'cuts', [(1, 0), (last - 1, last)])]
    ppermute x0 -> x33, starting transfers between devices: none -> 129 us  [the longest x15 94.3 us: slab_block(): parts.append(lax.ppermute(mine, 'cuts', pairs))]
    dot_general x2 -> x1, matrix products: 111 us -> 0.99 us  [slot_weights(): values = jnp.dot(one_hot, occ_levels, precision=lax.Precision.HIGHEST)]
    pallas_call x0 -> x16, Pallas kernels: none -> 58.4 us  [the longest x10 45.2 us: product(): pl.pallas_call(functools.partial(product_kernel, shape, always, base is n...]
    all_to_all x2 -> x0, blocking collectives: 50.3 us -> none  [the longest x1 29.9 us: shards(): lax.all_to_all(spread, 'cuts', split_axis=1, concat_axis=0, tiled=True)]
    all_to_all x0 -> x1, waiting for transfers between devices: none -> 15.3 us  [spread(): return lax.all_to_all(rows, 'row', split_axis=0, concat_axis=0, tiled=True)]
    reshape x2 -> x0, local copies, waits for them, and re-layouts: 8.61 us -> none  [the longest x1 8.28 us: shards(): panels.reshape(row_devices, cut_count, strip, owned).transpose(1, 0, 2, 3)]
  transfers between devices with their start and end apart: 2 -> 36, of which waited for: 2 -> 15; matrix products, arithmetic and copies ran while one was open for 2% -> 2% of each run, Pallas kernels for 0% -> 15%
where the time goes in v1:
time: 390 us; the launch traced here: 385 us
  waiting for transfers between devices  166 us (43%)
  starting transfers between devices  134 us (34%)
  Pallas kernels  58.4 us (15%)
  between operations  14.7 us (4%)
  local copies, waits for them, and re-layouts  6.78 us (2%)
    ppermute x15, starting transfers between devices, slab_block(): parts.append(lax.ppermute(mine, 'cuts', pairs))  94.3 us
    ppermute x6, waiting for transfers between devices, slab_block(): sents[tile] = lax.ppermute(served, 'cuts', [(1, 0), (last - 1, last)])  85.7 us
    pallas_call x10, Pallas kernels, product(): pl.pallas_call(functools.partial(product_kernel, shape, always, base is n...  45.2 us
    ppermute x3, waiting for transfers between devices, slab_block(): lax.ppermute(down[-1], 'cuts', [(i + 1, i) for i in range(last - step + 1)])  39.5 us
    ppermute x3, waiting for transfers between devices, slab_block(): own.append(lax.ppermute(piece, 'cuts', pairs))  19.4 us
    all_to_all x1, waiting for transfers between devices, spread(): return lax.all_to_all(rows, 'row', split_axis=0, concat_axis=0, tiled=True)  15.3 us
    pallas_call x6, Pallas kernels, place(): pl.pallas_call(functools.partial(place_kernel, tiles), in_specs=[pl.Block...  13.2 us
    ppermute x3, starting transfers between devices, slab_block(): lax.ppermute(up[-1], 'cuts', [(i, i + 1) for i in range(step - 1, last)])  10.5 us
  transfers between devices with their start and end apart: 36, of which 15 were waited for; matrix products, arithmetic and copies ran while one was open for 2% of the time, Pallas kernels for 15%

profile of v1, /device:TPU:0, one launch (start us, length us, event | category | flops | bytes accessed | tf_op | source)
XLA Modules:
  0.0 384.9 jit_solution(3039793352987886727)
XLA Ops:
  10.6 5.2 %all-to-all-start = ((f32[8,64,512]{2,1,0:T(8,128)}), f32[8,64,512]{2,1,0:T(8,128)S(1)}, u32[]{:S(2)}, u32[]{:S(2)}) async-start(f32[8,64,512]{2,1,0:T(8,128)} %broadcast_multiply_fusion), calls=%async_computation | async-start | bytes 2097152 | tf_op jit(solution)/shard_map/all_to_all | solution.py:205
  16.0 15.3 %all-to-all-done = f32[8,64,512]{2,1,0:T(8,128)S(1)} async-done(((f32[8,64,512]{2,1,0:T(8,128)}), f32[8,64,512]{2,1,0:T(8,128)S(1)}, u32[]{:S(2)}, u32[]{:S(2)}) %all-to-all-start) | async-done | bytes 1048608 | tf_op jit(solution)/shard_map/all_to_all | solution.py:205
  36.1 6.5 %collective-permute-done = f32[128,512]{1,0:T(8,128)S(1)} collective-permute-done((f32[128,512]{1,0:T(8,128)S(1)}, f32[128,512]{1,0:T(8,128)S(1)}, u32[]{:S(2)}, u32[]{:S(2)}) %collective-permute-start) | collective-permute-done | bytes 262176 | tf_op jit(solution)/shard_map/ppermute | solution.py:227
  44.3 11.1 %collective-permute-done.2 = f32[128,512]{1,0:T(8,128)S(1)} collective-permute-done((f32[128,512]{1,0:T(8,128)S(1)}, f32[128,512]{1,0:T(8,128)S(1)}, u32[]{:S(2)}, u32[]{:S(2)}) %collective-permute-start.2) | collective-permute-done | bytes 262176 | tf_op jit(solution)/shard_map/ppermute | solution.py:227
  58.6 5.3 %collective-permute-start.26 = (f32[128,512]{1,0:T(8,128)S(1)}, f32[128,512]{1,0:T(8,128)S(1)}, u32[]{:S(2)}, u32[]{:S(2)}) collective-permute-start(f32[128,512]{1,0:T(8,128)S(1)} %get-tuple-element.10), channel_id=1, source_target_pairs={{0,16},{24,8},{1,17},{25,9},{2,18},{26,10},{3,19},{27,11},{4,20},{... | collective-permute-start | bytes 786440 | tf_op jit(solution)/shard_map/ppermute | solution.py:225
  64.0 4.3 %collective-permute-done.26 = f32[128,512]{1,0:T(8,128)S(1)} collective-permute-done((f32[128,512]{1,0:T(8,128)S(1)}, f32[128,512]{1,0:T(8,128)S(1)}, u32[]{:S(2)}, u32[]{:S(2)}) %collective-permute-start.26) | collective-permute-done | bytes 262176 | tf_op jit(solution)/shard_map/ppermute | solution.py:225
  70.6 7.2 %collective-permute-start.18 = (f32[512,512]{1,0:T(8,128)S(1)}, f32[512,512]{1,0:T(8,128)S(1)}, u32[]{:S(2)}, u32[]{:S(2)}) collective-permute-start(f32[512,512]{1,0:T(8,128)S(1)} %bitcast.27), channel_id=1, source_target_pairs={{0,8},{8,16},{16,24},{1,9},{9,17},{17,25},{2,10},{10,18},{18,26},{... | collective-permute-start | bytes 3145736 | tf_op jit(solution)/shard_map/ppermute | solution.py:200
  77.8 18.3 %collective-permute-done.19.refs_4_.refs_11_ = f32[512,512]{1,0:T(8,128)S(1)} collective-permute-done((f32[512,512]{1,0:T(8,128)S(1)}, f32[512,512]{1,0:T(8,128)S(1)}, u32[]{:S(2)}, u32[]{:S(2)}) %collective-permute-start.19) | collective-permute-done | bytes 1048608 | tf_op jit(solution)/shard_map/ppermute | solution.py:201
  99.1 20.5 %collective-permute-done.20.refs_6_.refs_13_ = f32[512,512]{1,0:T(8,128)} collective-permute-done((f32[512,512]{1,0:T(8,128)S(1)}, f32[512,512]{1,0:T(8,128)}, u32[]{:S(2)}, u32[]{:S(2)}) %collective-permute-start.20) | collective-permute-done | bytes 1048608 | tf_op jit(solution)/shard_map/ppermute | solution.py:201
  123.9 5.6 %collective-permute-start.15 = (f32[512,512]{1,0:T(8,128)S(1)}, f32[512,512]{1,0:T(8,128)S(1)}, u32[]{:S(2)}, u32[]{:S(2)}) collective-permute-start(f32[512,512]{1,0:T(8,128)S(1)} %concatenate.10.refs_0_.refs_4_), channel_id=1, source_target_pairs={{0,8},{8,16},{1,9},{9,17},{2,10},{10,18},{3,11},{11,19},{4,12},{12... | collective-permute-start | bytes 3145736 | tf_op jit(solution)/shard_map/ppermute | solution.py:238
  130.2 8.2 %collective-permute-start.17 = (f32[512,512]{1,0:T(8,128)S(1)}, f32[512,512]{1,0:T(8,128)}, u32[]{:S(2)}, u32[]{:S(2)}) collective-permute-start(f32[512,512]{1,0:T(8,128)S(1)} %concatenate.10.refs_0_.refs_4_), channel_id=1, source_target_pairs={{0,16},{24,8},{1,17},{25,9},{2,18},{26,10},{3,19},{27,11},{4,20},{... | collective-permute-start | bytes 3145736 | tf_op jit(solution)/shard_map/ppermute | solution.py:238
  139.0 3.0 fusion.4
  144.1 4.3 %collective-permute-start.11 = (f32[256,512]{1,0:T(8,128)}, f32[256,512]{1,0:T(8,128)}, u32[]{:S(2)}, u32[]{:S(2)}) collective-permute-start(f32[256,512]{1,0:T(8,128)} %get-tuple-element.6.refs_0_), channel_id=1, source_target_pairs={{0,16},{24,8},{1,17},{25,9},{2,18},{26,10},{3,19},{27,11},{4,20},{... | collective-permute-start | bytes 1572872 | tf_op jit(solution)/shard_map/ppermute | solution.py:238
  148.4 16.9 %product.10.refs_8_ = f32[1024,2048]{1,0:T(8,128)} custom-call(s32[2]{0:T(128)} %iota_multiply_fusion.tiles, s32[1]{0:T(128)} %bitcast.flag, f32[1024,2048]{1,0:T(8,128)} %bitcast.15, f32[512,512]{1,0:T(8,128)} %bitcast.28, f32[512,512]{1,0:T(8,128)} %copy-done.7, f32[512,512]{1,0:T(8,128)} %collective-permute-done.21.refs_2_.refs_9_, ...), custom_call_target="tpu_custom_call" | custom-call | flops 6442450944 | bytes 14680064 | tf_op jit(solution)/shard_map/product/pallas_call | solution.py:118
  165.3 17.8 %collective-permute-start.12 = (f32[256,512]{1,0:T(8,128)}, f32[256,512]{1,0:T(8,128)}, u32[]{:S(2)}, u32[]{:S(2)}) collective-permute-start(f32[256,512]{1,0:T(8,128)} %get-tuple-element.5.refs_4_.refs_0_), channel_id=1, source_target_pairs={{0,8},{8,16},{1,9},{9,17},{2,10},{10,18},{3,11},{11,19},{4,12},{12... | collective-permute-start | bytes 1572872 | tf_op jit(solution)/shard_map/ppermute | solution.py:238
  184.5 4.9 %collective-permute-start.9 = (f32[256,512]{1,0:T(8,128)}, f32[256,512]{1,0:T(8,128)}, u32[]{:S(2)}, u32[]{:S(2)}) collective-permute-start(f32[256,512]{1,0:T(8,128)} %get-tuple-element.6.refs_0_), channel_id=1, source_target_pairs={{0,8},{8,16},{1,9},{9,17},{2,10},{10,18},{3,11},{11,19},{4,12},{12... | collective-permute-start | bytes 1572872 | tf_op jit(solution)/shard_map/ppermute | solution.py:238
  192.0 14.5 %collective-permute-start.14 = (f32[256,512]{1,0:T(8,128)S(1)}, f32[256,512]{1,0:T(8,128)S(1)}, u32[]{:S(2)}, u32[]{:S(2)}) collective-permute-start(f32[256,512]{1,0:T(8,128)S(1)} %copy-done.10), channel_id=1, source_target_pairs={{0,16},{24,8},{1,17},{25,9},{2,18},{26,10},{3,19},{27,11},{4,20},{... | collective-permute-start | bytes 1572872 | tf_op jit(solution)/shard_map/ppermute | solution.py:238
  212.4 12.8 %collective-permute-start.5 = (f32[256,512]{1,0:T(8,128)S(1)}, f32[256,512]{1,0:T(8,128)}, u32[]{:S(2)}, u32[]{:S(2)}) collective-permute-start(f32[256,512]{1,0:T(8,128)S(1)} %copy-done.9), channel_id=1, source_target_pairs={{0,16},{24,8},{1,17},{25,9},{2,18},{26,10},{3,19},{27,11},{4,20},{... | collective-permute-start | bytes 1572872 | tf_op jit(solution)/shard_map/ppermute | solution.py:238
  225.2 2.6 product.16
  227.9 6.7 %collective-permute-start.6 = (f32[256,512]{1,0:T(8,128)S(1)}, f32[256,512]{1,0:T(8,128)}, u32[]{:S(2)}, u32[]{:S(2)}) collective-permute-start(f32[256,512]{1,0:T(8,128)S(1)} %copy-done.8), channel_id=1, source_target_pairs={{0,8},{8,16},{1,9},{9,17},{2,10},{10,18},{3,11},{11,19},{4,12},{12... | collective-permute-start | bytes 1572872 | tf_op jit(solution)/shard_map/ppermute | solution.py:238
  235.3 12.0 %collective-permute-start.8 = (f32[256,512]{1,0:T(8,128)S(1)}, f32[256,512]{1,0:T(8,128)}, u32[]{:S(2)}, u32[]{:S(2)}) collective-permute-start(f32[256,512]{1,0:T(8,128)S(1)} %copy-done.8), channel_id=1, source_target_pairs={{0,16},{24,8},{1,17},{25,9},{2,18},{26,10},{3,19},{27,11},{4,20},{... | collective-permute-start | bytes 1572872 | tf_op jit(solution)/shard_map/ppermute | solution.py:238
  247.3 2.6 product.17
  261.2 2.7 product.19
  263.9 4.2 %product.11.refs_8_ = f32[1024,2048]{1,0:T(8,128)} custom-call(s32[2]{0:T(128)} %constant.57.clone.tiles, s32[1]{0:T(128)} %bitcast.flag, f32[1024,2048]{1,0:T(8,128)} %bitcast.16, f32[512,512]{1,0:T(8,128)} %copy-done.2, f32[512,512]{1,0:T(8,128)} %copy-done.4, f32[512,512]{1,0:T(8,128)} %copy-done.5, ...), custom_call_target="tpu_custom_call", output_to_operand_aliasing={{}: (11, {})} | custom-call | flops 6442450944 | bytes 14680064 | tf_op jit(solution)/shard_map/product/pallas_call | solution.py:118
  268.1 10.9 %collective-permute-done.27.sent_ref = f32[1024,256]{1,0:T(8,128)S(1)} collective-permute-done((f32[1024,256]{1,0:T(8,128)}, f32[1024,256]{1,0:T(8,128)S(1)}, u32[]{:S(2)}, u32[]{:S(2)}) %collective-permute-start.27) | collective-permute-done | bytes 1048608 | tf_op jit(solution)/shard_map/ppermute | solution.py:244
  280.6 4.2 %product.12.refs_8_ = f32[1024,2048]{1,0:T(8,128)} custom-call(s32[2]{0:T(128)} %constant.58.clone.tiles, s32[1]{0:T(128)} %bitcast.flag, f32[1024,2048]{1,0:T(8,128)} %bitcast.17, f32[256,512]{1,0:T(8,128)} %get-tuple-element.6.refs_0_, f32[256,512]{1,0:T(8,128)} %collective-permute-done.9.refs_1_, ...), custom_call_target="tpu_custom_call", output_to_operand_aliasing={{}: (11, {})} | custom-call | flops 6442450944 | bytes 14680064 | tf_op jit(solution)/shard_map/product/pallas_call | solution.py:118
  284.8 4.2 %product.13.base_ref = f32[1024,2048]{1,0:T(8,128)} custom-call(s32[2]{0:T(128)} %constant.59.clone.tiles, s32[1]{0:T(128)} %bitcast.flag, f32[1024,2048]{1,0:T(8,128)} %bitcast.18, f32[256,512]{1,0:T(8,128)} %get-tuple-element.8.refs_0_, f32[256,512]{1,0:T(8,128)} %copy-done.14, f32[256,512]{1,0:T(8,128)} %copy-done.15, ...), custom_call_target="tpu_custom_call", output_to_operand_aliasing={{}: (11, {})} | custom-call | flops 6442450944 | bytes 14680064 | tf_op jit(solution)/shard_map/product/pallas_call | solution.py:118
  291.3 10.2 %collective-permute-done.28.sent_ref = f32[1024,256]{1,0:T(8,128)S(1)} collective-permute-done((f32[1024,256]{1,0:T(8,128)}, f32[1024,256]{1,0:T(8,128)S(1)}, u32[]{:S(2)}, u32[]{:S(2)}) %collective-permute-start.28) | collective-permute-done | bytes 1048608 | tf_op jit(solution)/shard_map/ppermute | solution.py:244
  304.7 19.4 %collective-permute-done.29.sent_ref = f32[1024,256]{1,0:T(8,128)} collective-permute-done((f32[1024,256]{1,0:T(8,128)}, f32[1024,256]{1,0:T(8,128)}, u32[]{:S(2)}, u32[]{:S(2)}) %collective-permute-start.29) | collective-permute-done | bytes 1048608 | tf_op jit(solution)/shard_map/ppermute | solution.py:244
  326.3 20.3 %collective-permute-done.30.sent_ref = f32[1024,256]{1,0:T(8,128)} collective-permute-done((f32[1024,256]{1,0:T(8,128)}, f32[1024,256]{1,0:T(8,128)}, u32[]{:S(2)}, u32[]{:S(2)}) %collective-permute-start.30) | collective-permute-done | bytes 1048608 | tf_op jit(solution)/shard_map/ppermute | solution.py:244
  348.8 15.9 %collective-permute-done.31.sent_ref = f32[1024,256]{1,0:T(8,128)} collective-permute-done((f32[1024,256]{1,0:T(8,128)}, f32[1024,256]{1,0:T(8,128)}, u32[]{:S(2)}, u32[]{:S(2)}) %collective-permute-start.31) | collective-permute-done | bytes 1048608 | tf_op jit(solution)/shard_map/ppermute | solution.py:244
  366.9 9.0 %collective-permute-done.32.sent_ref = f32[1024,256]{1,0:T(8,128)} collective-permute-done((f32[1024,256]{1,0:T(8,128)}, f32[1024,256]{1,0:T(8,128)}, u32[]{:S(2)}, u32[]{:S(2)}) %collective-permute-start.32) | collective-permute-done | bytes 1048608 | tf_op jit(solution)/shard_map/ppermute | solution.py:244
  (102 shorter events, 63.8 us)
Async XLA Ops:
  10.6 20.6 %all-to-all-start = ((f32[8,64,512]{2,1,0:T(8,128)}), f32[8,64,512]{2,1,0:T(8,128)S(1)}, u32[]{:S(2)}, u32[]{:S(2)}) async-start(f32[8,64,512]{2,1,0:T(8,128)} %broadcast_multiply_fusion), calls=%async_computation | async-start | bytes 2097152 | tf_op jit(solution)/shard_map/all_to_all | solution.py:205
  15.8 132.5 %all-gather.3.cloned.1.call-start = ((), (), s32[]{:S(2)}) async-start(), calls=%async_computation.1 | async-start | bytes 9437184 | tf_op jit(solution)/shard_map/all_gather | solution.py:213
  33.0 11.3 %collective-permute-start.1 = (f32[128,512]{1,0:T(8,128)S(1)}, f32[128,512]{1,0:T(8,128)S(1)}, u32[]{:S(2)}, u32[]{:S(2)}) collective-permute-start(f32[128,512]{1,0:T(8,128)S(1)} %get-tuple-element.14), channel_id=1, source_target_pairs={{0,24},{8,0},{16,8},{24,16},{1,25},{9,1},{17,9},{25,17},{2,26},{10... | collective-permute-start | bytes 786440 | tf_op jit(solution)/shard_map/ppermute | solution.py:227
  35.3 20.2 %collective-permute-start.2 = (f32[128,512]{1,0:T(8,128)S(1)}, f32[128,512]{1,0:T(8,128)S(1)}, u32[]{:S(2)}, u32[]{:S(2)}) collective-permute-start(f32[128,512]{1,0:T(8,128)S(1)} %get-tuple-element.13), channel_id=1, source_target_pairs={{0,16},{8,24},{16,0},{24,8},{1,17},{9,25},{17,1},{25,9},{2,18},{10... | collective-permute-start | bytes 786440 | tf_op jit(solution)/shard_map/ppermute | solution.py:227
  56.6 132.9 %all-gather.5.cloned.1.call-start = ((), (), s32[]{:S(2)}) async-start(), calls=%async_computation.2 | async-start | bytes 9437184 | tf_op jit(solution)/shard_map/all_gather | solution.py:213
  69.3 26.8 %collective-permute-start.19 = (f32[512,512]{1,0:T(8,128)S(1)}, f32[512,512]{1,0:T(8,128)S(1)}, u32[]{:S(2)}, u32[]{:S(2)}) collective-permute-start(f32[512,512]{1,0:T(8,128)S(1)} %bitcast.26), channel_id=1, source_target_pairs={{8,0},{16,8},{24,16},{9,1},{17,9},{25,17},{10,2},{18,10},{26,18},{... | collective-permute-start | bytes 3145736 | tf_op jit(solution)/shard_map/ppermute | solution.py:201
  70.6 26.8 %collective-permute-start.18 = (f32[512,512]{1,0:T(8,128)S(1)}, f32[512,512]{1,0:T(8,128)S(1)}, u32[]{:S(2)}, u32[]{:S(2)}) collective-permute-start(f32[512,512]{1,0:T(8,128)S(1)} %bitcast.27), channel_id=1, source_target_pairs={{0,8},{8,16},{16,24},{1,9},{9,17},{17,25},{2,10},{10,18},{18,26},{... | collective-permute-start | bytes 3145736 | tf_op jit(solution)/shard_map/ppermute | solution.py:200
  96.1 23.6 %collective-permute-start.20 = (f32[512,512]{1,0:T(8,128)S(1)}, f32[512,512]{1,0:T(8,128)}, u32[]{:S(2)}, u32[]{:S(2)}) collective-permute-start(f32[512,512]{1,0:T(8,128)S(1)} %collective-permute-done.19.refs_4_.refs_11_), channel_id=1, source_target_pairs={{8,0},{16,8},{9,1},{17,9},{10,2},{18,10},{11,3},{19,11},{12,4},{20... | collective-permute-start | bytes 3145736 | tf_op jit(solution)/shard_map/ppermute | solution.py:201
  97.4 23.6 %collective-permute-start.22 = (f32[512,512]{1,0:T(8,128)S(1)}, f32[512,512]{1,0:T(8,128)}, u32[]{:S(2)}, u32[]{:S(2)}) collective-permute-start(f32[512,512]{1,0:T(8,128)S(1)} %collective-permute-done.18.refs_1_.refs_8_), channel_id=1, source_target_pairs={{8,16},{16,24},{9,17},{17,25},{10,18},{18,26},{11,19},{19,27},{12,... | collective-permute-start | bytes 3145736 | tf_op jit(solution)/shard_map/ppermute | solution.py:200
  119.7 22.9 %collective-permute-start.21 = (f32[512,512]{1,0:T(8,128)}, f32[512,512]{1,0:T(8,128)}, u32[]{:S(2)}, u32[]{:S(2)}) collective-permute-start(f32[512,512]{1,0:T(8,128)} %collective-permute-done.20.refs_6_.refs_13_), channel_id=1, source_target_pairs={{8,0},{9,1},{10,2},{11,3},{12,4},{13,5},{14,6},{15,7}} | collective-permute-start | bytes 3145736 | tf_op jit(solution)/shard_map/ppermute | solution.py:201
  121.0 23.1 %collective-permute-start.23 = (f32[512,512]{1,0:T(8,128)}, f32[512,512]{1,0:T(8,128)}, u32[]{:S(2)}, u32[]{:S(2)}) collective-permute-start(f32[512,512]{1,0:T(8,128)} %collective-permute-done.22.refs_5_.refs_12_), channel_id=1, source_target_pairs={{16,24},{17,25},{18,26},{19,27},{20,28},{21,29},{22,30},{23,31}} | collective-permute-start | bytes 3145736 | tf_op jit(solution)/shard_map/ppermute | solution.py:200
  123.9 41.3 %collective-permute-start.15 = (f32[512,512]{1,0:T(8,128)S(1)}, f32[512,512]{1,0:T(8,128)S(1)}, u32[]{:S(2)}, u32[]{:S(2)}) collective-permute-start(f32[512,512]{1,0:T(8,128)S(1)} %concatenate.10.refs_0_.refs_4_), channel_id=1, source_target_pairs={{0,8},{8,16},{1,9},{9,17},{2,10},{10,18},{3,11},{11,19},{4,12},{12... | collective-permute-start | bytes 3145736 | tf_op jit(solution)/shard_map/ppermute | solution.py:238
  129.5 53.6 %collective-permute-start.16 = (f32[512,512]{1,0:T(8,128)S(1)}, f32[512,512]{1,0:T(8,128)S(1)}, u32[]{:S(2)}, u32[]{:S(2)}) collective-permute-start(f32[512,512]{1,0:T(8,128)S(1)} %concatenate.10.refs_0_.refs_4_), channel_id=1, source_target_pairs={{16,8},{24,16},{17,9},{25,17},{18,10},{26,18},{19,11},{27,19},{20,... | collective-permute-start | bytes 3145736 | tf_op jit(solution)/shard_map/ppermute | solution.py:238
  130.2 54.3 %collective-permute-start.17 = (f32[512,512]{1,0:T(8,128)S(1)}, f32[512,512]{1,0:T(8,128)}, u32[]{:S(2)}, u32[]{:S(2)}) collective-permute-start(f32[512,512]{1,0:T(8,128)S(1)} %concatenate.10.refs_0_.refs_4_), channel_id=1, source_target_pairs={{0,16},{24,8},{1,17},{25,9},{2,18},{26,10},{3,19},{27,11},{4,20},{... | collective-permute-start | bytes 3145736 | tf_op jit(solution)/shard_map/ppermute | solution.py:238
  142.6 49.4 %collective-permute-start.10 = (f32[256,512]{1,0:T(8,128)}, f32[256,512]{1,0:T(8,128)}, u32[]{:S(2)}, u32[]{:S(2)}) collective-permute-start(f32[256,512]{1,0:T(8,128)} %get-tuple-element.6.refs_0_), channel_id=1, source_target_pairs={{16,8},{24,16},{17,9},{25,17},{18,10},{26,18},{19,11},{27,19},{20,... | collective-permute-start | bytes 1572872 | tf_op jit(solution)/shard_map/ppermute | solution.py:238
  144.1 62.4 %collective-permute-start.11 = (f32[256,512]{1,0:T(8,128)}, f32[256,512]{1,0:T(8,128)}, u32[]{:S(2)}, u32[]{:S(2)}) collective-permute-start(f32[256,512]{1,0:T(8,128)} %get-tuple-element.6.refs_0_), channel_id=1, source_target_pairs={{0,16},{24,8},{1,17},{25,9},{2,18},{26,10},{3,19},{27,11},{4,20},{... | collective-permute-start | bytes 1572872 | tf_op jit(solution)/shard_map/ppermute | solution.py:238
  165.3 46.2 %collective-permute-start.12 = (f32[256,512]{1,0:T(8,128)}, f32[256,512]{1,0:T(8,128)}, u32[]{:S(2)}, u32[]{:S(2)}) collective-permute-start(f32[256,512]{1,0:T(8,128)} %get-tuple-element.5.refs_4_.refs_0_), channel_id=1, source_target_pairs={{0,8},{8,16},{1,9},{9,17},{2,10},{10,18},{3,11},{11,19},{4,12},{12... | collective-permute-start | bytes 1572872 | tf_op jit(solution)/shard_map/ppermute | solution.py:238
  183.1 44.8 %collective-permute-start.13 = (f32[256,512]{1,0:T(8,128)}, f32[256,512]{1,0:T(8,128)}, u32[]{:S(2)}, u32[]{:S(2)}) collective-permute-start(f32[256,512]{1,0:T(8,128)} %get-tuple-element.5.refs_4_.refs_0_), channel_id=1, source_target_pairs={{16,8},{24,16},{17,9},{25,17},{18,10},{26,18},{19,11},{27,19},{20,... | collective-permute-start | bytes 1572872 | tf_op jit(solution)/shard_map/ppermute | solution.py:238
  184.5 27.9 %collective-permute-start.9 = (f32[256,512]{1,0:T(8,128)}, f32[256,512]{1,0:T(8,128)}, u32[]{:S(2)}, u32[]{:S(2)}) collective-permute-start(f32[256,512]{1,0:T(8,128)} %get-tuple-element.6.refs_0_), channel_id=1, source_target_pairs={{0,8},{8,16},{1,9},{9,17},{2,10},{10,18},{3,11},{11,19},{4,12},{12... | collective-permute-start | bytes 1572872 | tf_op jit(solution)/shard_map/ppermute | solution.py:238
  192.0 42.6 %collective-permute-start.14 = (f32[256,512]{1,0:T(8,128)S(1)}, f32[256,512]{1,0:T(8,128)S(1)}, u32[]{:S(2)}, u32[]{:S(2)}) collective-permute-start(f32[256,512]{1,0:T(8,128)S(1)} %copy-done.10), channel_id=1, source_target_pairs={{0,16},{24,8},{1,17},{25,9},{2,18},{26,10},{3,19},{27,11},{4,20},{... | collective-permute-start | bytes 1572872 | tf_op jit(solution)/shard_map/ppermute | solution.py:238
  206.5 28.8 %collective-permute-start.3 = (f32[256,512]{1,0:T(8,128)S(1)}, f32[256,512]{1,0:T(8,128)S(1)}, u32[]{:S(2)}, u32[]{:S(2)}) collective-permute-start(f32[256,512]{1,0:T(8,128)S(1)} %copy-done.9), channel_id=1, source_target_pairs={{0,8},{8,16},{1,9},{9,17},{2,10},{10,18},{3,11},{11,19},{4,12},{12... | collective-permute-start | bytes 1572872 | tf_op jit(solution)/shard_map/ppermute | solution.py:238
  211.6 38.3 %collective-permute-start.4 = (f32[256,512]{1,0:T(8,128)S(1)}, f32[256,512]{1,0:T(8,128)S(1)}, u32[]{:S(2)}, u32[]{:S(2)}) collective-permute-start(f32[256,512]{1,0:T(8,128)S(1)} %copy-done.9), channel_id=1, source_target_pairs={{16,8},{24,16},{17,9},{25,17},{18,10},{26,18},{19,11},{27,19},{20,... | collective-permute-start | bytes 1572872 | tf_op jit(solution)/shard_map/ppermute | solution.py:238
  212.4 38.8 %collective-permute-start.5 = (f32[256,512]{1,0:T(8,128)S(1)}, f32[256,512]{1,0:T(8,128)}, u32[]{:S(2)}, u32[]{:S(2)}) collective-permute-start(f32[256,512]{1,0:T(8,128)S(1)} %copy-done.9), channel_id=1, source_target_pairs={{0,16},{24,8},{1,17},{25,9},{2,18},{26,10},{3,19},{27,11},{4,20},{... | collective-permute-start | bytes 1572872 | tf_op jit(solution)/shard_map/ppermute | solution.py:238
  227.9 27.3 %collective-permute-start.6 = (f32[256,512]{1,0:T(8,128)S(1)}, f32[256,512]{1,0:T(8,128)}, u32[]{:S(2)}, u32[]{:S(2)}) collective-permute-start(f32[256,512]{1,0:T(8,128)S(1)} %copy-done.8), channel_id=1, source_target_pairs={{0,8},{8,16},{1,9},{9,17},{2,10},{10,18},{3,11},{11,19},{4,12},{12... | collective-permute-start | bytes 1572872 | tf_op jit(solution)/shard_map/ppermute | solution.py:238
  234.6 21.8 %collective-permute-start.7 = (f32[256,512]{1,0:T(8,128)S(1)}, f32[256,512]{1,0:T(8,128)S(1)}, u32[]{:S(2)}, u32[]{:S(2)}) collective-permute-start(f32[256,512]{1,0:T(8,128)S(1)} %copy-done.8), channel_id=1, source_target_pairs={{16,8},{24,16},{17,9},{25,17},{18,10},{26,18},{19,11},{27,19},{20,... | collective-permute-start | bytes 1572872 | tf_op jit(solution)/shard_map/ppermute | solution.py:238
  235.3 24.6 %collective-permute-start.8 = (f32[256,512]{1,0:T(8,128)S(1)}, f32[256,512]{1,0:T(8,128)}, u32[]{:S(2)}, u32[]{:S(2)}) collective-permute-start(f32[256,512]{1,0:T(8,128)S(1)} %copy-done.8), channel_id=1, source_target_pairs={{0,16},{24,8},{1,17},{25,9},{2,18},{26,10},{3,19},{27,11},{4,20},{... | collective-permute-start | bytes 1572872 | tf_op jit(solution)/shard_map/ppermute | solution.py:238
  249.9 29.2 %collective-permute-start.27 = (f32[1024,256]{1,0:T(8,128)}, f32[1024,256]{1,0:T(8,128)S(1)}, u32[]{:S(2)}, u32[]{:S(2)}) collective-permute-start(f32[1024,256]{1,0:T(8,128)} %product.14), channel_id=1, source_target_pairs={{8,0},{16,24},{9,1},{17,25},{10,2},{18,26},{11,3},{19,27},{12,4},{... | collective-permute-start | bytes 3145736 | tf_op jit(solution)/shard_map/ppermute | solution.py:244
  251.2 50.3 %collective-permute-start.28 = (f32[1024,256]{1,0:T(8,128)}, f32[1024,256]{1,0:T(8,128)S(1)}, u32[]{:S(2)}, u32[]{:S(2)}) collective-permute-start(f32[1024,256]{1,0:T(8,128)} %product.15), channel_id=1, source_target_pairs={{8,0},{16,24},{9,1},{17,25},{10,2},{18,26},{11,3},{19,27},{12,4},{... | collective-permute-start | bytes 3145736 | tf_op jit(solution)/shard_map/ppermute | solution.py:244
  255.1 69.0 %collective-permute-start.29 = (f32[1024,256]{1,0:T(8,128)}, f32[1024,256]{1,0:T(8,128)}, u32[]{:S(2)}, u32[]{:S(2)}) collective-permute-start(f32[1024,256]{1,0:T(8,128)} %product.16), channel_id=1, source_target_pairs={{8,0},{16,24},{9,1},{17,25},{10,2},{18,26},{11,3},{19,27},{12,4},{... | collective-permute-start | bytes 3145736 | tf_op jit(solution)/shard_map/ppermute | solution.py:244
  256.4 90.1 %collective-permute-start.30 = (f32[1024,256]{1,0:T(8,128)}, f32[1024,256]{1,0:T(8,128)}, u32[]{:S(2)}, u32[]{:S(2)}) collective-permute-start(f32[1024,256]{1,0:T(8,128)} %product.17), channel_id=1, source_target_pairs={{8,0},{16,24},{9,1},{17,25},{10,2},{18,26},{11,3},{19,27},{12,4},{... | collective-permute-start | bytes 3145736 | tf_op jit(solution)/shard_map/ppermute | solution.py:244
  259.9 104.7 %collective-permute-start.31 = (f32[1024,256]{1,0:T(8,128)}, f32[1024,256]{1,0:T(8,128)}, u32[]{:S(2)}, u32[]{:S(2)}) collective-permute-start(f32[1024,256]{1,0:T(8,128)} %product.18), channel_id=1, source_target_pairs={{8,0},{16,24},{9,1},{17,25},{10,2},{18,26},{11,3},{19,27},{12,4},{... | collective-permute-start | bytes 3145736 | tf_op jit(solution)/shard_map/ppermute | solution.py:244
  279.1 96.8 %collective-permute-start.32 = (f32[1024,256]{1,0:T(8,128)}, f32[1024,256]{1,0:T(8,128)}, u32[]{:S(2)}, u32[]{:S(2)}) collective-permute-start(f32[1024,256]{1,0:T(8,128)} %product.19), channel_id=1, source_target_pairs={{8,0},{16,24},{9,1},{17,25},{10,2},{18,26},{11,3},{19,27},{12,4},{... | collective-permute-start | bytes 3145736 | tf_op jit(solution)/shard_map/ppermute | solution.py:244
  (21 other events, 371.7 us)
Sparse Core Ops, SparseCore 0:
  56.7 54.5 all-gather.2
  113.2 54.2 all-gather.4

commit v2 on v1

--- a/solution.py
+++ b/solution.py
@@ -11,8 +11,10 @@
 BLOCK = 1024
 SLAB_SUB = 256
 TILE = 256
-SIZES = (2, 1, 1, 1, 1)
+OWNED = 2
+SIZES = (1, 1, 1, 1, 1, 1)
 STRIDE = 32
+STEP = 64
 PIECES = 8
 
 
@@ -54,14 +56,14 @@
 
         for index, tile_parts in enumerate(parts):
 
-            @pl.when(step == index)
+            @pl.when(step == index if len(parts) > 1 else step >= 0)
             def _():
                 for q, terms in enumerate(tile_parts):
                     at = slice(q * depth, (q + 1) * depth)
 
-                    @pl.loop(0, TILE // STRIDE)
+                    @pl.loop(0, TILE // STEP)
                     def _(j):
-                        rows = pl.ds(pl.multiple_of(j * STRIDE, STRIDE), STRIDE)
+                        rows = pl.ds(pl.multiple_of(j * STEP, STEP), STEP)
                         value = functools.reduce(jnp.add, [term[rows, :] for term in terms])
                         b_both[0, rows, at], b_both[1, rows, at] = split(value)
 
@@ -81,11 +83,9 @@
         dot = functools.partial(
             lax.dot_general, dimension_numbers=dims, preferred_element_type=jnp.float32
         )
-        out_ref[...] = dot(a_both[0], b_both[0])
-
-        @pl.loop(1, 3)
-        def _(term):
-            out_ref[...] += dot(a_both[term % 2], b_both[term // 2])
+        out_ref[...] = (
+            dot(a_both[0], b_both[0]) + dot(a_both[1], b_both[0]) + dot(a_both[0], b_both[1])
+        )
 
     if always:
         multiply()
@@ -96,20 +96,29 @@
 def product(rows, parts, flag, tiles, all_columns, always=False, base=None):
     owned, depth = rows.shape
     slots = parts[0][0][0][0].shape[1]
-    shape = [[len(terms) for terms in tile_parts] for tile_parts in parts]
+    same = all(
+        array is first and block == index
+        for index, tile_parts in enumerate(parts)
+        for terms, first_terms in zip(tile_parts, parts[0])
+        for (array, block), (first, _) in zip(terms, first_terms)
+    )
+    shown = parts[:1] if same else parts
+    shape = [[len(terms) for terms in tile_parts] for tile_parts in shown]
     operands = [rows]
     in_specs = [pl.BlockSpec(memory_space=pl.ANY)]
-    for tile_parts in parts:
+    for tile_parts in shown:
         for terms in tile_parts:
             for array, block in terms:
                 operands.append(array)
-                in_specs.append(
-                    pl.BlockSpec(
+                if same:
+                    spec = pl.BlockSpec((TILE, slots), lambda i, t, f: (i, 0))
+                else:
+                    spec = pl.BlockSpec(
                         (TILE, slots),
                         lambda i, t, f, block=block: (block, 0),
                         pipeline_mode=pl.Buffered(1),
                     )
-                )
+                in_specs.append(spec)
     aliases = {}
     if base is not None:
         aliases = {2 + len(operands): 0}
@@ -187,7 +196,7 @@
     row_devices = lax.axis_size("row")
     cut = lax.axis_index("cuts")
     last = cuts - 1
-    turns = [0, 1, last] + list(range(2, last))
+    turns = [0, 1, 3, 2] if cuts == 4 else list(range(cuts))
     at_end = ((cut == 0) | (cut == last)).astype(jnp.int32).reshape(1)
 
     weights = slot_weights(slice_counts, occ_index, occ_levels)
@@ -195,11 +204,21 @@
     picked = blocks[:, :SLAB_SUB, :].reshape(-1, slot_count)
     halves = row_devices // cuts
 
-    up, down = [picked], [picked]
-    for step in range(1, cuts):
-        up.append(lax.ppermute(up[-1], "cuts", [(i, i + 1) for i in range(step - 1, last)]))
-        down.append(lax.ppermute(down[-1], "cuts", [(i + 1, i) for i in range(last - step + 1)]))
-    every = [(picked,)] + [(up[turn], down[cuts - turn]) for turn in turns[1:]]
+    def moved(array, pairs):
+        return lax.ppermute(array, "cuts", pairs)
+
+    swap, outward = [(1, 2), (2, 1)], [(1, 0), (2, 3)]
+    if cuts == 4:
+        beside = moved(picked, [(i, i ^ 1) for i in range(cuts)])
+        across = moved(picked, swap)
+        onward = moved(beside, swap)
+        every = [
+            (picked,), (beside,), (across, moved(onward, outward)), (onward, moved(across, outward))
+        ]
+    else:
+        every = [(picked,)]
+        for turn in turns[1:]:
+            every.append((moved(picked, [(i, i ^ turn) for i in range(cuts)]),))
 
     def spread(rows):
         return lax.all_to_all(rows, "row", split_axis=0, concat_axis=0, tiled=True)
@@ -219,23 +238,26 @@
     strips = spread(picked * weights[None, :])
     other, own = [to_plane(strips, end_of(cut))], [to_plane(strips, cut)]
     for turn in turns[1:]:
-        pairs = [(i, (i + turn) % cuts) for i in range(cuts)]
+        pairs = [(i, i ^ turn) for i in range(cuts)]
         inner = [(i, j) for i, j in pairs if j in (1, last - 1)]
-        piece = to_plane(strips, end_of((cut + turn) % cuts))
-        other.append(lax.ppermute(piece, "cuts", inner))
-        piece = to_plane(strips, (cut + turn) % cuts)
-        own.append(lax.ppermute(piece, "cuts", pairs))
+        other.append(moved(to_plane(strips, end_of(cut ^ turn)), inner))
+        own.append(moved(to_plane(strips, cut ^ turn), pairs))
     other = gathered(jnp.concatenate(other, axis=1))
     own = gathered(jnp.concatenate(own, axis=1))
 
     groups, tile_parts = unpicked_groups(row_count), {}
     for group in groups:
         mine = jnp.concatenate([eigvecs[t * TILE : (t + 1) * TILE] for t in group], axis=0)
-        parts = [mine]
-        for turn in turns[1:]:
-            pairs = [(i, (i + turn) % cuts) for i in range(cuts)]
-            pairs = [(i, j) for i, j in pairs if 0 < j < last]
-            parts.append(lax.ppermute(mine, "cuts", pairs))
+        if cuts == 4:
+            beside = moved(mine, [(0, 1), (3, 2)])
+            across = moved(mine, swap)
+            parts = [mine, beside, across, moved(beside, swap)]
+        else:
+            parts = [mine]
+            for turn in turns[1:]:
+                pairs = [(i, i ^ turn) for i in range(cuts)]
+                pairs = [(i, j) for i, j in pairs if 0 < j < last]
+                parts.append(moved(mine, pairs))
         for block, tile in enumerate(group):
             tile_parts[tile] = [[(part, block)] for part in parts]
     sents = {}
@@ -266,7 +288,7 @@
 
 def owned_groups(row_count):
     tiles = [t for group in unpicked_groups(row_count) for t in group]
-    return [tiles[i : i + 2] for i in range(0, len(tiles), 2)]
+    return [g for g in (tiles[:OWNED], tiles[OWNED:]) if g]
 
 
 def solution(mesh):

time: 390 us -> 366 us (0.938)
  starting transfers between devices: 134 us -> 106 us
  waiting for transfers between devices: 166 us -> 176 us
  Pallas kernels: 58.4 us -> 54.3 us
    ppermute x27 -> x29, starting transfers between devices: 121 us -> 93 us  [moved(): return lax.ppermute(array, 'cuts', pairs)]
    ppermute x6, waiting for transfers between devices: 85.7 us -> 111 us  [slab_block(): sents[tile] = lax.ppermute(served, 'cuts', [(1, 0), (last - 1, last)])]
    ppermute x27 -> x29, waiting for transfers between devices: 65.3 us -> 49.7 us  [moved(): return lax.ppermute(array, 'cuts', pairs)]
    pallas_call x10 -> x9, Pallas kernels: 45.2 us -> 41.1 us  [product(): pl.pallas_call(functools.partial(product_kernel, shape, always, base is n...]
  transfers between devices with their start and end apart: 36 -> 38, of which waited for: 15 -> 14; matrix products, arithmetic and copies ran while one was open for 2% -> 1% of each run, Pallas kernels for 15% -> 14%
where the time goes in v2:
time: 366 us; the launch traced here: 363 us
  waiting for transfers between devices  176 us (48%)
  starting transfers between devices  106 us (29%)
  Pallas kernels  54.3 us (15%)
  between operations  14.7 us (4%)
  local copies, waits for them, and re-layouts  7.03 us (2%)
  other arithmetic  3.9 us (1%)
    ppermute x6, waiting for transfers between devices, slab_block(): sents[tile] = lax.ppermute(served, 'cuts', [(1, 0), (last - 1, last)])  111 us
    ppermute x29, starting transfers between devices, moved(): return lax.ppermute(array, 'cuts', pairs)  93 us
    ppermute x29, waiting for transfers between devices, moved(): return lax.ppermute(array, 'cuts', pairs)  49.7 us
    pallas_call x9, Pallas kernels, product(): pl.pallas_call(functools.partial(product_kernel, shape, always, base is n...  41.1 us
    all_to_all x1, waiting for transfers between devices, spread(): return lax.all_to_all(rows, 'row', split_axis=0, concat_axis=0, tiled=True)  15.3 us
    pallas_call x6, Pallas kernels, place(): pl.pallas_call(functools.partial(place_kernel, tiles), in_specs=[pl.Block...  13.2 us
    ppermute x6, starting transfers between devices, slab_block(): sents[tile] = lax.ppermute(served, 'cuts', [(1, 0), (last - 1, last)])  7.95 us
  transfers between devices with their start and end apart: 38, of which 14 were waited for; matrix products, arithmetic and copies ran while one was open for 1% of the time, Pallas kernels for 14%

profile of v2, /device:TPU:0, one launch (start us, length us, event | category | flops | bytes accessed | tf_op | source)
XLA Modules:
  0.0 363.3 jit_solution(3086006512214644596)
XLA Ops:
  10.7 5.2 %all-to-all-start = ((f32[8,64,512]{2,1,0:T(8,128)}), f32[8,64,512]{2,1,0:T(8,128)S(1)}, u32[]{:S(2)}, u32[]{:S(2)}) async-start(f32[8,64,512]{2,1,0:T(8,128)} %broadcast_multiply_fusion), calls=%async_computation | async-start | bytes 2097152 | tf_op jit(solution)/shard_map/all_to_all | solution.py:224
  15.9 15.3 %all-to-all-done = f32[8,64,512]{2,1,0:T(8,128)S(1)} async-done(((f32[8,64,512]{2,1,0:T(8,128)}), f32[8,64,512]{2,1,0:T(8,128)S(1)}, u32[]{:S(2)}, u32[]{:S(2)}) %all-to-all-start) | async-done | bytes 1048608 | tf_op jit(solution)/shard_map/all_to_all | solution.py:224
  35.7 6.2 %collective-permute-done = f32[128,512]{1,0:T(8,128)S(1)} collective-permute-done((f32[128,512]{1,0:T(8,128)S(1)}, f32[128,512]{1,0:T(8,128)S(1)}, u32[]{:S(2)}, u32[]{:S(2)}) %collective-permute-start) | collective-permute-done | bytes 262176 | tf_op jit(solution)/shard_map/ppermute | solution.py:208
  41.8 5.5 %collective-permute-done.1 = f32[128,512]{1,0:T(8,128)S(1)} collective-permute-done((f32[128,512]{1,0:T(8,128)S(1)}, f32[128,512]{1,0:T(8,128)S(1)}, u32[]{:S(2)}, u32[]{:S(2)}) %collective-permute-start.1) | collective-permute-done | bytes 262176 | tf_op jit(solution)/shard_map/ppermute | solution.py:208
  47.3 8.5 %collective-permute-done.2 = f32[128,512]{1,0:T(8,128)S(1)} collective-permute-done((f32[128,512]{1,0:T(8,128)S(1)}, f32[128,512]{1,0:T(8,128)S(1)}, u32[]{:S(2)}, u32[]{:S(2)}) %collective-permute-start.2) | collective-permute-done | bytes 262176 | tf_op jit(solution)/shard_map/ppermute | solution.py:208
  59.3 4.0 %collective-permute-start.28 = (f32[128,512]{1,0:T(8,128)S(1)}, f32[128,512]{1,0:T(8,128)S(1)}, u32[]{:S(2)}, u32[]{:S(2)}) collective-permute-start(f32[128,512]{1,0:T(8,128)S(1)} %get-tuple-element.12), channel_id=1, source_target_pairs={{0,16},{24,8},{1,17},{25,9},{2,18},{26,10},{3,19},{27,11},{4,20},{... | collective-permute-start | bytes 786440 | tf_op jit(solution)/shard_map/ppermute | solution.py:208
  64.1 4.1 %collective-permute-done.28 = f32[128,512]{1,0:T(8,128)S(1)} collective-permute-done((f32[128,512]{1,0:T(8,128)S(1)}, f32[128,512]{1,0:T(8,128)S(1)}, u32[]{:S(2)}, u32[]{:S(2)}) %collective-permute-start.28) | collective-permute-done | bytes 262176 | tf_op jit(solution)/shard_map/ppermute | solution.py:208
  69.3 3.6 %collective-permute-start.21 = (f32[512,512]{1,0:T(8,128)S(1)}, f32[512,512]{1,0:T(8,128)S(1)}, u32[]{:S(2)}, u32[]{:S(2)}) collective-permute-start(f32[512,512]{1,0:T(8,128)S(1)} %bitcast.21), channel_id=1, source_target_pairs={{0,8},{8,0},{16,24},{24,16},{1,9},{9,1},{17,25},{25,17},{2,10},{10... | collective-permute-start | bytes 3145736 | tf_op jit(solution)/shard_map/ppermute | solution.py:208
  74.6 18.8 %collective-permute-done.21.refs_1_ = f32[512,512]{1,0:T(8,128)S(1)} collective-permute-done((f32[512,512]{1,0:T(8,128)S(1)}, f32[512,512]{1,0:T(8,128)S(1)}, u32[]{:S(2)}, u32[]{:S(2)}) %collective-permute-start.21) | collective-permute-done | bytes 1048608 | tf_op jit(solution)/shard_map/ppermute | solution.py:208
  95.1 3.4 fusion.4
  98.5 5.4 %collective-permute-start.15 = (f32[256,512]{1,0:T(8,128)S(1)}, f32[256,512]{1,0:T(8,128)S(1)}, u32[]{:S(2)}, u32[]{:S(2)}) collective-permute-start(f32[256,512]{1,0:T(8,128)S(1)} %get-tuple-element.10.refs_0_), channel_id=1, source_target_pairs={{0,8},{24,16},{1,9},{25,17},{2,10},{26,18},{3,11},{27,19},{4,12},{... | collective-permute-start | bytes 1572872 | tf_op jit(solution)/shard_map/ppermute | solution.py:208
  106.5 17.3 %collective-permute-start.18 = (f32[256,512]{1,0:T(8,128)S(1)}, f32[256,512]{1,0:T(8,128)S(1)}, u32[]{:S(2)}, u32[]{:S(2)}) collective-permute-start(f32[256,512]{1,0:T(8,128)S(1)} %get-tuple-element.5.refs_4_.refs_0_), channel_id=1, source_target_pairs={{0,8},{24,16},{1,9},{25,17},{2,10},{26,18},{3,11},{27,19},{4,12},{... | collective-permute-start | bytes 1572872 | tf_op jit(solution)/shard_map/ppermute | solution.py:208
  125.9 5.8 %collective-permute-done.18.refs_5_.refs_1_ = f32[256,512]{1,0:T(8,128)S(1)} collective-permute-done((f32[256,512]{1,0:T(8,128)S(1)}, f32[256,512]{1,0:T(8,128)S(1)}, u32[]{:S(2)}, u32[]{:S(2)}) %collective-permute-start.18) | collective-permute-done | bytes 524320 | tf_op jit(solution)/shard_map/ppermute | solution.py:208
  131.7 5.2 %collective-permute-start.9 = (f32[256,512]{1,0:T(8,128)}, f32[256,512]{1,0:T(8,128)}, u32[]{:S(2)}, u32[]{:S(2)}) collective-permute-start(f32[256,512]{1,0:T(8,128)} %get-tuple-element.7.refs_8_.refs_0_), channel_id=1, source_target_pairs={{0,8},{24,16},{1,9},{25,17},{2,10},{26,18},{3,11},{27,19},{4,12},{... | collective-permute-start | bytes 1572872 | tf_op jit(solution)/shard_map/ppermute | solution.py:208
  136.9 5.7 %collective-permute-start.3 = (f32[256,512]{1,0:T(8,128)}, f32[256,512]{1,0:T(8,128)}, u32[]{:S(2)}, u32[]{:S(2)}) collective-permute-start(f32[256,512]{1,0:T(8,128)} %get-tuple-element.9.refs_0_), channel_id=1, source_target_pairs={{0,8},{24,16},{1,9},{25,17},{2,10},{26,18},{3,11},{27,19},{4,12},{... | collective-permute-start | bytes 1572872 | tf_op jit(solution)/shard_map/ppermute | solution.py:208
  142.6 6.9 %collective-permute-start.6 = (f32[256,512]{1,0:T(8,128)}, f32[256,512]{1,0:T(8,128)}, u32[]{:S(2)}, u32[]{:S(2)}) collective-permute-start(f32[256,512]{1,0:T(8,128)} %get-tuple-element.8.refs_4_.refs_0_), channel_id=1, source_target_pairs={{0,8},{24,16},{1,9},{25,17},{2,10},{26,18},{3,11},{27,19},{4,12},{... | collective-permute-start | bytes 1572872 | tf_op jit(solution)/shard_map/ppermute | solution.py:208
  152.4 14.8 %product.9.refs_8_ = f32[1024,2048]{1,0:T(8,128)} custom-call(s32[2]{0:T(128)} %iota_multiply_fusion.tiles, s32[1]{0:T(128)} %bitcast.flag, f32[1024,2048]{1,0:T(8,128)} %bitcast.16, f32[512,512]{1,0:T(8,128)} %bitcast.23, f32[512,512]{1,0:T(8,128)} %copy-done.14, f32[512,512]{1,0:T(8,128)} %collective-permute-done.22.refs_2_, ...), custom_call_target="tpu_custom_call" | custom-call | flops 6442450944 | bytes 14680064 | tf_op jit(solution)/shard_map/product/pallas_call | solution.py:127
  168.9 2.7 product.12
  172.4 18.4 %collective-permute-start.12 = (f32[256,512]{1,0:T(8,128)}, f32[256,512]{1,0:T(8,128)}, u32[]{:S(2)}, u32[]{:S(2)}) collective-permute-start(f32[256,512]{1,0:T(8,128)} %get-tuple-element.6.refs_12_.refs_0_), channel_id=1, source_target_pairs={{0,8},{24,16},{1,9},{25,17},{2,10},{26,18},{3,11},{27,19},{4,12},{... | collective-permute-start | bytes 1572872 | tf_op jit(solution)/shard_map/ppermute | solution.py:208
  192.3 2.6 product.13
  197.9 2.6 product.14
  204.8 2.6 product.15
  210.0 2.6 product.16
  215.4 2.6 product.17
  218.0 4.2 %product.10.refs_16_ = f32[1024,2048]{1,0:T(8,128)} custom-call(s32[2]{0:T(128)} %constant.30.clone.tiles, s32[1]{0:T(128)} %bitcast.flag, f32[1024,2048]{1,0:T(8,128)} %bitcast.17, f32[256,512]{1,0:T(8,128)} %copy-done.4, f32[256,512]{1,0:T(8,128)} %copy-done.8, f32[256,512]{1,0:T(8,128)} %copy-done.10, ...), custom_call_target="tpu_custom_call", output_to_operand_aliasing={{}: (11, {})} | custom-call | flops 6442450944 | bytes 14680064 | tf_op jit(solution)/shard_map/product/pallas_call | solution.py:127
  222.2 26.3 %collective-permute-done.29.sent_ref = f32[1024,256]{1,0:T(8,128)S(1)} collective-permute-done((f32[1024,256]{1,0:T(8,128)}, f32[1024,256]{1,0:T(8,128)S(1)}, u32[]{:S(2)}, u32[]{:S(2)}) %collective-permute-start.29) | collective-permute-done | bytes 1048608 | tf_op jit(solution)/shard_map/ppermute | solution.py:266
  249.8 6.5 %product.11.base_ref = f32[1024,2048]{1,0:T(8,128)} custom-call(s32[4]{0:T(128)} %constant.31.clone.tiles, s32[1]{0:T(128)} %bitcast.flag, f32[1024,2048]{1,0:T(8,128)} %bitcast.18, f32[256,512]{1,0:T(8,128)} %get-tuple-element.9.refs_0_, f32[256,512]{1,0:T(8,128)} %collective-permute-done.3.refs_1_, ...), custom_call_target="tpu_custom_call", output_to_operand_aliasing={{}: (19, {})} | custom-call | flops 12884901888 | bytes 20971520 | tf_op jit(solution)/shard_map/product/pallas_call | solution.py:127
  258.5 12.5 %collective-permute-done.30.sent_ref = f32[1024,256]{1,0:T(8,128)S(1)} collective-permute-done((f32[1024,256]{1,0:T(8,128)}, f32[1024,256]{1,0:T(8,128)S(1)}, u32[]{:S(2)}, u32[]{:S(2)}) %collective-permute-start.30) | collective-permute-done | bytes 1048608 | tf_op jit(solution)/shard_map/ppermute | solution.py:266
  274.2 19.2 %collective-permute-done.31.sent_ref = f32[1024,256]{1,0:T(8,128)S(1)} collective-permute-done((f32[1024,256]{1,0:T(8,128)}, f32[1024,256]{1,0:T(8,128)S(1)}, u32[]{:S(2)}, u32[]{:S(2)}) %collective-permute-start.31) | collective-permute-done | bytes 1048608 | tf_op jit(solution)/shard_map/ppermute | solution.py:266
  296.7 19.3 %collective-permute-done.32.sent_ref = f32[1024,256]{1,0:T(8,128)} collective-permute-done((f32[1024,256]{1,0:T(8,128)}, f32[1024,256]{1,0:T(8,128)}, u32[]{:S(2)}, u32[]{:S(2)}) %collective-permute-start.32) | collective-permute-done | bytes 1048608 | tf_op jit(solution)/shard_map/ppermute | solution.py:266
  318.2 20.3 %collective-permute-done.33.sent_ref = f32[1024,256]{1,0:T(8,128)} collective-permute-done((f32[1024,256]{1,0:T(8,128)}, f32[1024,256]{1,0:T(8,128)}, u32[]{:S(2)}, u32[]{:S(2)}) %collective-permute-start.33) | collective-permute-done | bytes 1048608 | tf_op jit(solution)/shard_map/ppermute | solution.py:266
  340.7 13.5 %collective-permute-done.34.sent_ref = f32[1024,256]{1,0:T(8,128)} collective-permute-done((f32[1024,256]{1,0:T(8,128)}, f32[1024,256]{1,0:T(8,128)}, u32[]{:S(2)}, u32[]{:S(2)}) %collective-permute-start.34) | collective-permute-done | bytes 1048608 | tf_op jit(solution)/shard_map/ppermute | solution.py:266
  (106 shorter events, 57.1 us)
Async XLA Ops:
  10.7 20.6 %all-to-all-start = ((f32[8,64,512]{2,1,0:T(8,128)}), f32[8,64,512]{2,1,0:T(8,128)S(1)}, u32[]{:S(2)}, u32[]{:S(2)}) async-start(f32[8,64,512]{2,1,0:T(8,128)} %broadcast_multiply_fusion), calls=%async_computation | async-start | bytes 2097152 | tf_op jit(solution)/shard_map/all_to_all | solution.py:224
  15.9 136.6 %all-gather.3.cloned.1.call-start = ((), (), s32[]{:S(2)}) async-start(), calls=%async_computation.1 | async-start | bytes 9437184 | tf_op jit(solution)/shard_map/all_gather | solution.py:232
  33.1 14.2 %collective-permute-start.1 = (f32[128,512]{1,0:T(8,128)S(1)}, f32[128,512]{1,0:T(8,128)S(1)}, u32[]{:S(2)}, u32[]{:S(2)}) collective-permute-start(f32[128,512]{1,0:T(8,128)S(1)} %get-tuple-element.16), channel_id=1, source_target_pairs={{0,24},{8,16},{16,8},{24,0},{1,25},{9,17},{17,9},{25,1},{2,26},{10... | collective-permute-start | bytes 786440 | tf_op jit(solution)/shard_map/ppermute | solution.py:208
  35.6 20.2 %collective-permute-start.2 = (f32[128,512]{1,0:T(8,128)S(1)}, f32[128,512]{1,0:T(8,128)S(1)}, u32[]{:S(2)}, u32[]{:S(2)}) collective-permute-start(f32[128,512]{1,0:T(8,128)S(1)} %get-tuple-element.15), channel_id=1, source_target_pairs={{0,16},{8,24},{16,0},{24,8},{1,17},{9,25},{17,1},{25,9},{2,18},{10... | collective-permute-start | bytes 786440 | tf_op jit(solution)/shard_map/ppermute | solution.py:208
  56.9 112.0 %all-gather.5.cloned.1.call-start = ((), (), s32[]{:S(2)}) async-start(), calls=%async_computation.2 | async-start | bytes 9437184 | tf_op jit(solution)/shard_map/all_gather | solution.py:232
  69.3 24.1 %collective-permute-start.21 = (f32[512,512]{1,0:T(8,128)S(1)}, f32[512,512]{1,0:T(8,128)S(1)}, u32[]{:S(2)}, u32[]{:S(2)}) collective-permute-start(f32[512,512]{1,0:T(8,128)S(1)} %bitcast.21), channel_id=1, source_target_pairs={{0,8},{8,0},{16,24},{24,16},{1,9},{9,1},{17,25},{25,17},{2,10},{10... | collective-permute-start | bytes 3145736 | tf_op jit(solution)/shard_map/ppermute | solution.py:208
  73.0 31.0 %collective-permute-start.22 = (f32[512,512]{1,0:T(8,128)S(1)}, f32[512,512]{1,0:T(8,128)}, u32[]{:S(2)}, u32[]{:S(2)}) collective-permute-start(f32[512,512]{1,0:T(8,128)S(1)} %bitcast.22), channel_id=1, source_target_pairs={{8,16},{16,8},{9,17},{17,9},{10,18},{18,10},{11,19},{19,11},{12,20... | collective-permute-start | bytes 3145736 | tf_op jit(solution)/shard_map/ppermute | solution.py:208
  98.5 26.1 %collective-permute-start.15 = (f32[256,512]{1,0:T(8,128)S(1)}, f32[256,512]{1,0:T(8,128)S(1)}, u32[]{:S(2)}, u32[]{:S(2)}) collective-permute-start(f32[256,512]{1,0:T(8,128)S(1)} %get-tuple-element.10.refs_0_), channel_id=1, source_target_pairs={{0,8},{24,16},{1,9},{25,17},{2,10},{26,18},{3,11},{27,19},{4,12},{... | collective-permute-start | bytes 1572872 | tf_op jit(solution)/shard_map/ppermute | solution.py:208
  103.9 45.6 %collective-permute-start.25 = (f32[512,512]{1,0:T(8,128)}, f32[512,512]{1,0:T(8,128)}, u32[]{:S(2)}, u32[]{:S(2)}) collective-permute-start(f32[512,512]{1,0:T(8,128)} %collective-permute-done.22.refs_2_), channel_id=1, source_target_pairs={{8,0},{16,24},{9,1},{17,25},{10,2},{18,26},{11,3},{19,27},{12,4},{... | collective-permute-start | bytes 3145736 | tf_op jit(solution)/shard_map/ppermute | solution.py:208
  105.2 45.7 %collective-permute-start.24 = (f32[512,512]{1,0:T(8,128)}, f32[512,512]{1,0:T(8,128)}, u32[]{:S(2)}, u32[]{:S(2)}) collective-permute-start(f32[512,512]{1,0:T(8,128)} %collective-permute-done.23.refs_4_), channel_id=1, source_target_pairs={{8,0},{16,24},{9,1},{17,25},{10,2},{18,26},{11,3},{19,27},{12,4},{... | collective-permute-start | bytes 3145736 | tf_op jit(solution)/shard_map/ppermute | solution.py:208
  106.5 25.2 %collective-permute-start.18 = (f32[256,512]{1,0:T(8,128)S(1)}, f32[256,512]{1,0:T(8,128)S(1)}, u32[]{:S(2)}, u32[]{:S(2)}) collective-permute-start(f32[256,512]{1,0:T(8,128)S(1)} %get-tuple-element.5.refs_4_.refs_0_), channel_id=1, source_target_pairs={{0,8},{24,16},{1,9},{25,17},{2,10},{26,18},{3,11},{27,19},{4,12},{... | collective-permute-start | bytes 1572872 | tf_op jit(solution)/shard_map/ppermute | solution.py:208
  123.9 13.0 %collective-permute-start.16 = (f32[256,512]{1,0:T(8,128)S(1)}, f32[256,512]{1,0:T(8,128)S(1)}, u32[]{:S(2)}, u32[]{:S(2)}) collective-permute-start(f32[256,512]{1,0:T(8,128)S(1)} %get-tuple-element.10.refs_0_), channel_id=1, source_target_pairs={{8,16},{16,8},{9,17},{17,9},{10,18},{18,10},{11,19},{19,11},{12,20... | collective-permute-start | bytes 1572872 | tf_op jit(solution)/shard_map/ppermute | solution.py:208
  124.6 18.0 %collective-permute-start.19 = (f32[256,512]{1,0:T(8,128)S(1)}, f32[256,512]{1,0:T(8,128)S(1)}, u32[]{:S(2)}, u32[]{:S(2)}) collective-permute-start(f32[256,512]{1,0:T(8,128)S(1)} %get-tuple-element.5.refs_4_.refs_0_), channel_id=1, source_target_pairs={{8,16},{16,8},{9,17},{17,9},{10,18},{18,10},{11,19},{19,11},{12,20... | collective-permute-start | bytes 1572872 | tf_op jit(solution)/shard_map/ppermute | solution.py:208
  131.7 39.8 %collective-permute-start.9 = (f32[256,512]{1,0:T(8,128)}, f32[256,512]{1,0:T(8,128)}, u32[]{:S(2)}, u32[]{:S(2)}) collective-permute-start(f32[256,512]{1,0:T(8,128)} %get-tuple-element.7.refs_8_.refs_0_), channel_id=1, source_target_pairs={{0,8},{24,16},{1,9},{25,17},{2,10},{26,18},{3,11},{27,19},{4,12},{... | collective-permute-start | bytes 1572872 | tf_op jit(solution)/shard_map/ppermute | solution.py:208
  136.9 30.4 %collective-permute-start.3 = (f32[256,512]{1,0:T(8,128)}, f32[256,512]{1,0:T(8,128)}, u32[]{:S(2)}, u32[]{:S(2)}) collective-permute-start(f32[256,512]{1,0:T(8,128)} %get-tuple-element.9.refs_0_), channel_id=1, source_target_pairs={{0,8},{24,16},{1,9},{25,17},{2,10},{26,18},{3,11},{27,19},{4,12},{... | collective-permute-start | bytes 1572872 | tf_op jit(solution)/shard_map/ppermute | solution.py:208
  142.6 29.8 %collective-permute-start.6 = (f32[256,512]{1,0:T(8,128)}, f32[256,512]{1,0:T(8,128)}, u32[]{:S(2)}, u32[]{:S(2)}) collective-permute-start(f32[256,512]{1,0:T(8,128)} %get-tuple-element.8.refs_4_.refs_0_), channel_id=1, source_target_pairs={{0,8},{24,16},{1,9},{25,17},{2,10},{26,18},{3,11},{27,19},{4,12},{... | collective-permute-start | bytes 1572872 | tf_op jit(solution)/shard_map/ppermute | solution.py:208
  149.5 18.7 %collective-permute-start.17 = (f32[256,512]{1,0:T(8,128)S(1)}, f32[256,512]{1,0:T(8,128)}, u32[]{:S(2)}, u32[]{:S(2)}) collective-permute-start(f32[256,512]{1,0:T(8,128)S(1)} %collective-permute-done.15.refs_1_), channel_id=1, source_target_pairs={{8,16},{16,8},{9,17},{17,9},{10,18},{18,10},{11,19},{19,11},{12,20... | collective-permute-start | bytes 1572872 | tf_op jit(solution)/shard_map/ppermute | solution.py:208
  151.0 39.9 %collective-permute-start.20 = (f32[256,512]{1,0:T(8,128)S(1)}, f32[256,512]{1,0:T(8,128)}, u32[]{:S(2)}, u32[]{:S(2)}) collective-permute-start(f32[256,512]{1,0:T(8,128)S(1)} %collective-permute-done.18.refs_5_.refs_1_), channel_id=1, source_target_pairs={{8,16},{16,8},{9,17},{17,9},{10,18},{18,10},{11,19},{19,11},{12,20... | collective-permute-start | bytes 1572872 | tf_op jit(solution)/shard_map/ppermute | solution.py:208
  167.3 27.6 %collective-permute-start.4 = (f32[256,512]{1,0:T(8,128)}, f32[256,512]{1,0:T(8,128)S(1)}, u32[]{:S(2)}, u32[]{:S(2)}) collective-permute-start(f32[256,512]{1,0:T(8,128)} %get-tuple-element.9.refs_0_), channel_id=1, source_target_pairs={{8,16},{16,8},{9,17},{17,9},{10,18},{18,10},{11,19},{19,11},{12,20... | collective-permute-start | bytes 1572872 | tf_op jit(solution)/shard_map/ppermute | solution.py:208
  168.2 28.3 %collective-permute-start.5 = (f32[256,512]{1,0:T(8,128)}, f32[256,512]{1,0:T(8,128)S(1)}, u32[]{:S(2)}, u32[]{:S(2)}) collective-permute-start(f32[256,512]{1,0:T(8,128)} %collective-permute-done.3.refs_1_), channel_id=1, source_target_pairs={{8,16},{16,8},{9,17},{17,9},{10,18},{18,10},{11,19},{19,11},{12,20... | collective-permute-start | bytes 1572872 | tf_op jit(solution)/shard_map/ppermute | solution.py:208
  171.6 30.4 %collective-permute-start.7 = (f32[256,512]{1,0:T(8,128)S(1)}, f32[256,512]{1,0:T(8,128)S(1)}, u32[]{:S(2)}, u32[]{:S(2)}) collective-permute-start(f32[256,512]{1,0:T(8,128)S(1)} %copy-done.13), channel_id=1, source_target_pairs={{8,16},{16,8},{9,17},{17,9},{10,18},{18,10},{11,19},{19,11},{12,20... | collective-permute-start | bytes 1572872 | tf_op jit(solution)/shard_map/ppermute | solution.py:208
  172.4 28.1 %collective-permute-start.12 = (f32[256,512]{1,0:T(8,128)}, f32[256,512]{1,0:T(8,128)}, u32[]{:S(2)}, u32[]{:S(2)}) collective-permute-start(f32[256,512]{1,0:T(8,128)} %get-tuple-element.6.refs_12_.refs_0_), channel_id=1, source_target_pairs={{0,8},{24,16},{1,9},{25,17},{2,10},{26,18},{3,11},{27,19},{4,12},{... | collective-permute-start | bytes 1572872 | tf_op jit(solution)/shard_map/ppermute | solution.py:208
  190.8 12.6 %collective-permute-start.8 = (f32[256,512]{1,0:T(8,128)}, f32[256,512]{1,0:T(8,128)}, u32[]{:S(2)}, u32[]{:S(2)}) collective-permute-start(f32[256,512]{1,0:T(8,128)} %collective-permute-done.6.refs_5_.refs_1_), channel_id=1, source_target_pairs={{8,16},{16,8},{9,17},{17,9},{10,18},{18,10},{11,19},{19,11},{12,20... | collective-permute-start | bytes 1572872 | tf_op jit(solution)/shard_map/ppermute | solution.py:208
  195.0 12.4 %collective-permute-start.10 = (f32[256,512]{1,0:T(8,128)S(1)}, f32[256,512]{1,0:T(8,128)}, u32[]{:S(2)}, u32[]{:S(2)}) collective-permute-start(f32[256,512]{1,0:T(8,128)S(1)} %copy-done.12), channel_id=1, source_target_pairs={{8,16},{16,8},{9,17},{17,9},{10,18},{18,10},{11,19},{19,11},{12,20... | collective-permute-start | bytes 1572872 | tf_op jit(solution)/shard_map/ppermute | solution.py:208
  196.4 12.2 %collective-permute-start.11 = (f32[256,512]{1,0:T(8,128)}, f32[256,512]{1,0:T(8,128)}, u32[]{:S(2)}, u32[]{:S(2)}) collective-permute-start(f32[256,512]{1,0:T(8,128)} %collective-permute-done.9.refs_9_.refs_1_), channel_id=1, source_target_pairs={{8,16},{16,8},{9,17},{17,9},{10,18},{18,10},{11,19},{19,11},{12,20... | collective-permute-start | bytes 1572872 | tf_op jit(solution)/shard_map/ppermute | solution.py:208
  200.5 12.0 %collective-permute-start.13 = (f32[256,512]{1,0:T(8,128)}, f32[256,512]{1,0:T(8,128)}, u32[]{:S(2)}, u32[]{:S(2)}) collective-permute-start(f32[256,512]{1,0:T(8,128)} %get-tuple-element.6.refs_12_.refs_0_), channel_id=1, source_target_pairs={{8,16},{16,8},{9,17},{17,9},{10,18},{18,10},{11,19},{19,11},{12,20... | collective-permute-start | bytes 1572872 | tf_op jit(solution)/shard_map/ppermute | solution.py:208
  203.5 45.0 %collective-permute-start.29 = (f32[1024,256]{1,0:T(8,128)}, f32[1024,256]{1,0:T(8,128)S(1)}, u32[]{:S(2)}, u32[]{:S(2)}) collective-permute-start(f32[1024,256]{1,0:T(8,128)} %product.12), channel_id=1, source_target_pairs={{8,0},{16,24},{9,1},{17,25},{10,2},{18,26},{11,3},{19,27},{12,4},{... | collective-permute-start | bytes 3145736 | tf_op jit(solution)/shard_map/ppermute | solution.py:266
  207.3 63.6 %collective-permute-start.30 = (f32[1024,256]{1,0:T(8,128)}, f32[1024,256]{1,0:T(8,128)S(1)}, u32[]{:S(2)}, u32[]{:S(2)}) collective-permute-start(f32[1024,256]{1,0:T(8,128)} %product.13), channel_id=1, source_target_pairs={{8,0},{16,24},{9,1},{17,25},{10,2},{18,26},{11,3},{19,27},{12,4},{... | collective-permute-start | bytes 3145736 | tf_op jit(solution)/shard_map/ppermute | solution.py:266
  208.7 84.8 %collective-permute-start.31 = (f32[1024,256]{1,0:T(8,128)}, f32[1024,256]{1,0:T(8,128)S(1)}, u32[]{:S(2)}, u32[]{:S(2)}) collective-permute-start(f32[1024,256]{1,0:T(8,128)} %product.14), channel_id=1, source_target_pairs={{8,0},{16,24},{9,1},{17,25},{10,2},{18,26},{11,3},{19,27},{12,4},{... | collective-permute-start | bytes 3145736 | tf_op jit(solution)/shard_map/ppermute | solution.py:266
  212.5 103.5 %collective-permute-start.32 = (f32[1024,256]{1,0:T(8,128)}, f32[1024,256]{1,0:T(8,128)}, u32[]{:S(2)}, u32[]{:S(2)}) collective-permute-start(f32[1024,256]{1,0:T(8,128)} %product.15), channel_id=1, source_target_pairs={{8,0},{16,24},{9,1},{17,25},{10,2},{18,26},{11,3},{19,27},{12,4},{... | collective-permute-start | bytes 3145736 | tf_op jit(solution)/shard_map/ppermute | solution.py:266
  213.9 124.6 %collective-permute-start.33 = (f32[1024,256]{1,0:T(8,128)}, f32[1024,256]{1,0:T(8,128)}, u32[]{:S(2)}, u32[]{:S(2)}) collective-permute-start(f32[1024,256]{1,0:T(8,128)} %product.16), channel_id=1, source_target_pairs={{8,0},{16,24},{9,1},{17,25},{10,2},{18,26},{11,3},{19,27},{12,4},{... | collective-permute-start | bytes 3145736 | tf_op jit(solution)/shard_map/ppermute | solution.py:266
  248.5 105.7 %collective-permute-start.34 = (f32[1024,256]{1,0:T(8,128)}, f32[1024,256]{1,0:T(8,128)}, u32[]{:S(2)}, u32[]{:S(2)}) collective-permute-start(f32[1024,256]{1,0:T(8,128)} %product.17), channel_id=1, source_target_pairs={{8,0},{16,24},{9,1},{17,25},{10,2},{18,26},{11,3},{19,27},{12,4},{... | collective-permute-start | bytes 3145736 | tf_op jit(solution)/shard_map/ppermute | solution.py:266
  (24 other events, 512.6 us)
Sparse Core Ops, SparseCore 0:
  57.0 55.5 all-gather.2
  114.5 54.2 all-gather.4
